TPU v7x, 32 devices: a whole 2x2x4 slice. The times are simulated.
32 devices in a mesh: fsdp: 16 (over z, x, core), tp: 2 (over y).
Axes of the slice: x: 2, y: 2, z: 4, core: 2. Of those that a mesh axis runs over, the one named last changes fastest.
Arguments:
- hidden: bfloat16 [4096, 8192], P('fsdp'), may hold values from -6 to 6
- norm_gain: float32 [8192], replicated, may hold values from 0.6 to 6, as said below
- w_query: bfloat16 [8192, 4096], P('fsdp', 'tp'), may hold values from -0.09375 to 0.09375
- w_key: bfloat16 [8192, 512], P('fsdp'), may hold values from -0.09375 to 0.09375
- w_value: bfloat16 [8192, 512], P('fsdp'), may hold values from -0.0625 to 0.0625
- bias_query: bfloat16 [4096], P('tp'), may hold values from -3 to 3
- bias_key: bfloat16 [512], replicated, may hold values from -3 to 3
- bias_value: bfloat16 [512], replicated, may hold values from -3 to 3
- w_out: bfloat16 [4096, 8192], P('tp', 'fsdp'), may hold values from -0.09375 to 0.09375
- seq_lengths: int32 [4], replicated, may hold values from 1 to 3072, 4096 in all
Outputs:
- hidden_out: float32 [4096, 8192], P(('fsdp', 'tp'))
Inputs may be any that keep to these rules, and one draw needn't show every extreme that they name: `seq_lengths`: 4 sequences packed in order; the lengths sum to 4096 and the longest has exactly 3072 tokens. `norm_gain`: positive gains.
All inputs are finite; a program needn't handle non-finite values.
Results may differ from a plain program's by a relative error of at most 0.014.
The roundings to bfloat16 on the way count: a program that leaves them out, or rounds other values in their place, can miss the bound.
Values may be sent and summed in bfloat16 or wider, within the bound.
A program may use at most 128 MiB of HBM per device.

v0:
```python
import math

import jax
import jax.numpy as jnp
from jax import lax
from jax.sharding import PartitionSpec as P

HEAD = 128
QHEADS = 32
KVHEADS = 4


ROPE_BASE = 1000000.0
EPSILON = 1e-06
FLOOR = -1e30


def token_layout(seq_lengths, token_index):
    seq_ends = jnp.cumsum(seq_lengths)
    seq_starts = seq_ends - seq_lengths
    member = (token_index[:, None] >= seq_ends[None, :]).astype(jnp.int32)
    segment = jnp.sum(member, axis=1)
    one_hot = segment[:, None] == jnp.arange(seq_lengths.shape[0], dtype=jnp.int32)[None, :]
    seq_begin = jnp.sum(jnp.where(one_hot, seq_starts[None, :], 0), axis=1)
    return (segment, token_index - seq_begin)


def rotary(vectors, position):
    half_size = vectors.shape[-1] // 2
    frequency = jnp.exp(
        jnp.arange(half_size, dtype=jnp.float32) * (-2.0 * math.log(ROPE_BASE) / vectors.shape[-1])
    )
    angle = position.astype(jnp.float32)[:, None] * frequency[None, :]
    cos_table = jnp.concatenate([jnp.cos(angle), jnp.cos(angle)], axis=1)[:, None, :]
    sin_table = jnp.concatenate([jnp.sin(angle), jnp.sin(angle)], axis=1)[:, None, :]
    turned = jnp.concatenate([-vectors[..., half_size:], vectors[..., :half_size]], axis=-1)
    return vectors * cos_table + turned * sin_table


def shards(
    hidden, norm_gain, w_query, w_key, w_value, bias_query, bias_key, bias_value, w_out, seq_lengths
):
    tok_rows = hidden.shape[0]
    first_row = lax.axis_index("fsdp") * tok_rows
    local_index = first_row + jnp.arange(tok_rows, dtype=jnp.int32)
    segment, position = token_layout(seq_lengths, local_index)
    widened = hidden.astype(jnp.float32)
    scale = lax.rsqrt(jnp.mean(widened * widened, axis=1, keepdims=True) + EPSILON)
    normed = (widened * scale * norm_gain[None, :]).astype(jnp.bfloat16)
    query_cols = w_query.shape[1]
    local_heads = query_cols // HEAD
    group_size = QHEADS // KVHEADS
    local_kv = max(local_heads // group_size, 1)
    first_kv = lax.axis_index("tp") * local_heads // group_size
    key_cols = local_kv * HEAD
    key_part = lax.dynamic_slice_in_dim(w_key, first_kv * HEAD, key_cols, 1)
    value_part = lax.dynamic_slice_in_dim(w_value, first_kv * HEAD, key_cols, 1)
    key_bias = lax.dynamic_slice_in_dim(bias_key, first_kv * HEAD, key_cols, 0)
    value_bias = lax.dynamic_slice_in_dim(bias_value, first_kv * HEAD, key_cols, 0)
    pieces = (
        lax.all_gather(w_query, "fsdp", axis=0, tiled=True),
        lax.all_gather(key_part, "fsdp", axis=0, tiled=True),
        lax.all_gather(value_part, "fsdp", axis=0, tiled=True),
    )
    query, keys, values = tuple(
        (jnp.dot(normed, piece, preferred_element_type=jnp.float32) for piece in pieces)
    )
    query = rotary(
        (query + bias_query.astype(jnp.float32)[None, :]).reshape(tok_rows, -1, HEAD), position
    ).astype(jnp.bfloat16)
    keys = rotary(
        (keys + key_bias.astype(jnp.float32)[None, :]).reshape(tok_rows, -1, HEAD), position
    ).astype(jnp.bfloat16)
    values = (values + value_bias.astype(jnp.float32)[None, :]).astype(jnp.bfloat16)
    keys = keys.reshape(tok_rows, key_cols)
    per_kv = local_heads // local_kv
    query_grid = query.reshape(tok_rows, local_kv, per_kv, HEAD)
    start_state = (
        jnp.full((local_kv, per_kv, tok_rows), FLOOR, jnp.float32),
        jnp.zeros((local_kv, per_kv, tok_rows), jnp.float32),
        jnp.zeros((local_kv, per_kv, tok_rows, HEAD), jnp.float32),
    )
    key_piece = lax.all_gather(keys, "fsdp", axis=0, tiled=True)
    value_piece = lax.all_gather(values, "fsdp", axis=0, tiled=True)
    piece_rows = key_piece.shape[0]
    shard_count = max(piece_rows // tok_rows, 1)
    per_block = 1
    for divisor in range(1, 9):
        if shard_count % divisor == 0:
            per_block = divisor
    block_rows = min(per_block * tok_rows, piece_rows)
    block_count = piece_rows // block_rows

    def fold_block(block_number, carried):
        running_max, total, accumulated = carried
        offset = block_number * block_rows
        key_block = lax.dynamic_slice_in_dim(key_piece, offset, block_rows, 0).reshape(
            block_rows, local_kv, HEAD
        )
        value_block = lax.dynamic_slice_in_dim(value_piece, offset, block_rows, 0).reshape(
            block_rows, local_kv, HEAD
        )
        key_index = offset + jnp.arange(block_rows, dtype=jnp.int32)
        key_segment, unused = token_layout(seq_lengths, key_index)
        scores = jnp.einsum(
            "qkgd,nkd->kgqn", query_grid, key_block, preferred_element_type=jnp.float32
        ) * HEAD ** (-0.5)
        allowed = (
            (segment[:, None] == key_segment[None, :])
            & (local_index[:, None] >= key_index[None, :])
        )[None, None]
        scores = jnp.where(allowed, scores, FLOOR)
        new_max = jnp.maximum(running_max, jnp.max(scores, axis=3))
        weights = jnp.where(allowed, jnp.exp(scores - new_max[..., None]), 0.0)
        factor = jnp.exp(running_max - new_max)
        total = total * factor + jnp.sum(weights, axis=3)
        update = jnp.einsum(
            "kgqn,nkd->kgqd",
            weights.astype(jnp.bfloat16),
            value_block,
            preferred_element_type=jnp.float32,
        )
        accumulated = accumulated * factor[..., None] + update
        return (new_max, total, accumulated)

    final_state = lax.fori_loop(0, block_count, fold_block, start_state)
    mixed = final_state[2] / final_state[1][..., None]
    attended = jnp.transpose(mixed, (2, 0, 1, 3)).reshape(tok_rows, query_cols).astype(jnp.bfloat16)
    share_rows = tok_rows // lax.axis_size("tp")
    own_rows = lax.dynamic_slice_in_dim(
        hidden, lax.axis_index("tp") * share_rows, share_rows, 0
    ).astype(jnp.float32)
    terms = jnp.dot(
        attended,
        lax.all_gather(w_out, "fsdp", axis=1, tiled=True),
        preferred_element_type=jnp.float32,
    )
    summed = lax.psum_scatter(
        terms.astype(jnp.bfloat16), "tp", scatter_dimension=0, tiled=True
    ).astype(jnp.float32)
    return own_rows + summed


def solution(mesh):
    in_specs = (
        P("fsdp", None),
        P(),
        P("fsdp", "tp"),
        P("fsdp", None),
        P("fsdp", None),
        P("tp"),
        P(),
        P(),
        P("tp", "fsdp"),
        P(),
    )
    out_specs = P(("fsdp", "tp"), None)
    return jax.shard_map(shards, mesh=mesh, in_specs=in_specs, out_specs=out_specs, check_vma=False)
```

profile of v0, /device:TPU:0, one launch (start us, length us, event | category | flops | bytes accessed | tf_op | source)
XLA Modules:
  0.0 618.8 jit_solution(51648293795599105)
XLA Ops:
  6.5 1.0 copy-done
  7.6 0.7 constant_dynamic-slice_fusion.3
  8.4 1.7 constant_dynamic-slice_fusion.2
  10.2 0.7 all-gather.11.cloned.1.call-update
  10.9 0.8 reduce-window.9
  11.9 0.7 bitcast_subtract_fusion
  12.6 0.5 multiply_cosine_fusion
  13.2 0.1 pad_maximum_fusion.1
  13.7 3.1 fusion.15
  16.8 45.9 %all-gather.7.cloned.1.call-done = bf16[8192,256]{1,0:T(8,128)(2,1)} async-done(((bf16[512,256]{1,0:T(8,128)(2,1)}), bf16[8192,256]{1,0:T(8,128)(2,1)}) %all-gather.7.cloned.1.call-update) | async-done | bytes 4194320 | tf_op jit(solution)/shard_map/all_gather | solution.py:62
  62.7 5.6 convolution_add_fusion.2
  68.3 0.7 fusion.21
  69.2 44.6 %all-gather.13.cloned.1.call-done = bf16[8192,256]{1,0:T(8,128)(2,1)} async-done(((bf16[512,256]{1,0:T(8,128)(2,1)}), bf16[8192,256]{1,0:T(8,128)(2,1)}) %all-gather.13.cloned.1.call-update) | async-done | bytes 4194320 | tf_op jit(solution)/shard_map/all_gather | solution.py:63
  113.8 5.4 fusion.20
  119.3 0.5 all-gather.17.cloned.1.call-update
  119.8 0.2 reduce-scatter.2.cloned.1.call-start
  120.1 0.2 broadcast_in_dim.117
  120.3 161.7 %all-gather.11.cloned.1.call-done = bf16[8192,2048]{1,0:T(8,128)(2,1)} async-done(((bf16[512,2048]{1,0:T(8,128)(2,1)}), bf16[8192,2048]{1,0:T(8,128)(2,1)}) %all-gather.11.cloned.1.call-update) | async-done | bytes 33554448 | tf_op jit(solution)/shard_map/all_gather | solution.py:61
  282.0 16.5 %convolution_add_fusion = f32[256,2048]{1,0:T(8,128)S(1)} fusion(bf16[8192,2048]{1,0:T(8,128)(2,1)} %all-gather.11.cloned.1.call-done, f32[2048]{0:T(1024)S(1)} %convert_element_type.80, bf16[256,8192]{1,0:T(8,128)(2,1)} %param.12, f32[8192]{0:T(1024)S(1)} %copy-done.8, f32[256]{0:T(256)S(1)} %add_rsqrt_fusion), kind=kOutput, calls=%fused_computation.30 | convolution fusion | flops 8598847488 | bytes 39887872 | tf_op jit(solution)/shard_map/dot_general | solution.py:66
  298.5 1.9 copy.44
  300.3 3.1 slice_negate_fusion
  303.5 3.2 copy.45
  306.6 3.2 copy.46
  309.9 0.4 copy.57
  310.2 1.2 copy-done.3
  311.4 0.6 copy-done.4
  312.1 1.0 fusion.19
  313.1 12.0 %all-gather.9.cloned.1.call-done = bf16[4096,256]{0,1:T(8,128)(2,1)} async-done(((bf16[256,256]{0,1:T(8,128)(2,1)}), bf16[4096,256]{0,1:T(8,128)(2,1)}) %all-gather.9.cloned.1.call-update) | async-done | bytes 2097168 | tf_op jit(solution)/shard_map/all_gather | solution.py:83
  325.1 42.6 %all-gather.15.cloned.1.call-done = bf16[4096,256]{1,0:T(8,128)(2,1)} async-done(((bf16[256,256]{1,0:T(8,128)(2,1)}), bf16[4096,256]{1,0:T(8,128)(2,1)}) %all-gather.15.cloned.1.call-update) | async-done | bytes 2097168 | tf_op jit(solution)/shard_map/all_gather | solution.py:84
  367.6 104.9 %while.20 = (s32[]{:T(128)}, f32[2,8,256]{2,1,0:T(8,128)S(1)}, f32[2,8,256]{2,1,0:T(8,128)S(1)}, f32[2,8,256,128]{3,2,1,0:T(8,128)}, s32[256]{0:T(256)S(1)}, /*i...) while((s32[]{:T(128)}, f32[2,8,256]{2,1,0:T(8,128)S(1)}, ...), condition=%wide.region_9.10_spmd.clone, body=%wide.region_5.9_spmd.clone.sunk | while | flops 4407209984 | bytes 125086968 | solution.py:126
  367.6 1.3 constant_dynamic-slice_fusion.6
  369.1 1.4 compare_and_fusion.2
  370.5 15.2 %fusion.45 = (f32[2,8,256]{2,1,0:T(8,128)S(1)}, f32[2,2048,256,8]{2,1,3,0:T(8,128)}) fusion(pred[256,2048]{0,1:T(8,128)(4,1)S(1)} %compare_and_fusion.2, bf16[2048,2,128,1]{0,2,3,1:T(8,128)(2,1)S(1)} %bitcast.72, bf16[256,2,8,128]{3,0,2,1:T(8,128)(2,1)S(1)} %get-tuple-element.451), kind=kOutput, calls=%fused_computation.3.clone.1 | convolution fusion | flops 2172645376 | bytes 36192256 | tf_op jit(solution)/shard_map/while/body/eval_jaxpr/qkgd,nkd->kgqn/dot_general | solution.py:105
  385.7 15.3 %fusion.46 = f32[2,8,256]{2,1,0:T(8,128)S(1)} fusion(f32[2,2048,256,8]{2,1,3,0:T(8,128)} %get-tuple-element.413, f32[2,8,256]{2,1,0:T(8,128)S(1)} %select_maximum_fusion.2, pred[256,2048]{0,1:T(8,128)(4,1)S(1)} %compare_and_fusion.2), kind=kLoop, calls=%fused_computation.5.clone.1 | loop fusion | flops 41938944 | bytes 34111488 | tf_op jit(solution)/shard_map/while/body/eval_jaxpr/reduce_sum | solution.py:116
  401.2 1.4 copy.62
  402.6 17.6 %fusion.48 = f32[2,8,256,128]{3,2,1,0:T(8,128)} fusion(f32[2,8,256,128]{3,2,1,0:T(8,128)} %get-tuple-element.433, bf16[2048,2,128,1]{0,2,3,1:T(8,128)(2,1)} %bitcast.73, f32[2,2048,256,8]{2,1,3,0:T(8,128)} %get-tuple-element.413, f32[2,8,256]{2,1,0:T(8,128)S(1)} %select_maximum_fusion.2, pred[256,2048]{0,1:T(8,128)(4,1)S(1)} %compare_and_fusion.2, ...), kind=kOutput, calls=%fused_computation.9.clone.1 | convolution fusion | flops 2190999552 | bytes 39354368 | tf_op jit(solution)/shard_map/while/body/eval_jaxpr/kgqn,nkd->kgqd/dot_general | solution.py:117
  420.2 1.3 constant_dynamic-slice_fusion.6
  421.7 1.4 compare_and_fusion.2
  423.1 14.1 %fusion.45 = (f32[2,8,256]{2,1,0:T(8,128)S(1)}, f32[2,2048,256,8]{2,1,3,0:T(8,128)}) fusion(pred[256,2048]{0,1:T(8,128)(4,1)S(1)} %compare_and_fusion.2, bf16[2048,2,128,1]{0,2,3,1:T(8,128)(2,1)S(1)} %bitcast.72, bf16[256,2,8,128]{3,0,2,1:T(8,128)(2,1)S(1)} %get-tuple-element.451), kind=kOutput, calls=%fused_computation.3.clone.1 | convolution fusion | flops 2172645376 | bytes 36192256 | tf_op jit(solution)/shard_map/while/body/eval_jaxpr/qkgd,nkd->kgqn/dot_general | solution.py:105
  437.3 15.6 %fusion.46 = f32[2,8,256]{2,1,0:T(8,128)S(1)} fusion(f32[2,2048,256,8]{2,1,3,0:T(8,128)} %get-tuple-element.413, f32[2,8,256]{2,1,0:T(8,128)S(1)} %select_maximum_fusion.2, pred[256,2048]{0,1:T(8,128)(4,1)S(1)} %compare_and_fusion.2), kind=kLoop, calls=%fused_computation.5.clone.1 | loop fusion | flops 41938944 | bytes 34111488 | tf_op jit(solution)/shard_map/while/body/eval_jaxpr/reduce_sum | solution.py:116
  452.9 1.4 copy.62
  454.4 18.2 %fusion.48 = f32[2,8,256,128]{3,2,1,0:T(8,128)} fusion(f32[2,8,256,128]{3,2,1,0:T(8,128)} %get-tuple-element.433, bf16[2048,2,128,1]{0,2,3,1:T(8,128)(2,1)} %bitcast.73, f32[2,2048,256,8]{2,1,3,0:T(8,128)} %get-tuple-element.413, f32[2,8,256]{2,1,0:T(8,128)S(1)} %select_maximum_fusion.2, pred[256,2048]{0,1:T(8,128)(4,1)S(1)} %compare_and_fusion.2, ...), kind=kOutput, calls=%fused_computation.9.clone.1 | convolution fusion | flops 2190999552 | bytes 39354368 | tf_op jit(solution)/shard_map/while/body/eval_jaxpr/kgqn,nkd->kgqd/dot_general | solution.py:117
  472.6 2.1 copy.48
  474.7 1.2 divide_convert_fusion
  475.9 59.9 %all-gather.17.cloned.1.call-done = bf16[2048,8192]{1,0:T(8,128)(2,1)} async-done(((bf16[2048,512]{1,0:T(8,128)(2,1)}), bf16[2048,8192]{1,0:T(8,128)(2,1)}) %all-gather.17.cloned.1.call-update) | async-done | bytes 33554448 | tf_op jit(solution)/shard_map/all_gather | solution.py:135
  535.9 16.8 %convolution_convert_fusion = bf16[256,8192]{1,0:T(8,128)(2,1)} fusion(bf16[256,2048]{0,1:T(8,128)(2,1)} %bitcast.77, bf16[2048,8192]{1,0:T(8,128)(2,1)} %all-gather.17.cloned.1.call-done), kind=kOutput, calls=%fused_computation.25 | convolution fusion | flops 8592031744 | bytes 38797312 | tf_op jit(solution)/shard_map/dot_general | solution.py:133
  552.7 54.5 %reduce-scatter.2.cloned.1.call-done = bf16[128,8192]{1,0:T(8,128)(2,1)} async-done(((bf16[256,8192]{1,0:T(8,128)(2,1)}), bf16[128,8192]{1,0:T(8,128)(2,1)}) %reduce-scatter.2.cloned.1.call-update) | async-done | bytes 2097168 | tf_op jit(solution)/shard_map/reduce_scatter | solution.py:138
  607.2 4.8 convert_add_fusion
  (61 shorter events, 1.4 us)
Async XLA Ops:
  6.5 1.0 copy-start
  6.5 7.0 %copy-start.6 = (bf16[512]{0:T(512)(128)(2,1)S(1)}, bf16[512]{0:T(512)(128)(2,1)}, u32[]{:S(2)}) copy-start(bf16[512]{0:T(512)(128)(2,1)} %param.18) | copy-start | bytes 3076
  6.5 56.1 %all-gather.7.cloned.1.call-start = ((), (), s32[]{:S(2)}) async-start(), calls=%async_computation.1 | async-start | bytes 4456448 | tf_op jit(solution)/shard_map/all_gather | solution.py:62
  8.3 54.4 %copy-start.8 = (f32[8192]{0:T(1024)S(1)}, f32[8192]{0:T(1024)}, u32[]{:S(2)}) copy-start(f32[8192]{0:T(1024)} %param.13) | copy-start | bytes 98308
  8.3 105.4 %all-gather.13.cloned.1.call-start = ((), (), s32[]{:S(2)}) async-start(), calls=%async_computation.4 | async-start | bytes 4456448 | tf_op jit(solution)/shard_map/all_gather | solution.py:63
  10.1 271.9 %all-gather.11.cloned.1.call-start = ((), (), s32[]{:S(2)}) async-start(), calls=%async_computation.3 | async-start | bytes 35651584 | tf_op jit(solution)/shard_map/all_gather | solution.py:61
  10.9 314.2 %all-gather.9.cloned.1.call-start = ((), (), s32[]{:S(2)}) async-start(), calls=%async_computation.2 | async-start | bytes 2228224 | tf_op jit(solution)/shard_map/all_gather | solution.py:83
  16.8 52.3 %copy-start.7 = (bf16[512]{0:T(512)(128)(2,1)S(1)}, bf16[512]{0:T(512)(128)(2,1)}, u32[]{:S(2)}) copy-start(bf16[512]{0:T(512)(128)(2,1)} %param.19) | copy-start | bytes 3076
  69.0 298.6 %all-gather.15.cloned.1.call-start = ((), (), s32[]{:S(2)}) async-start(), calls=%async_computation.5 | async-start | bytes 2228224 | tf_op jit(solution)/shard_map/all_gather | solution.py:84
  69.2 50.9 %copy-start.5 = (bf16[2048]{0:T(1024)(128)(2,1)S(1)}, bf16[2048]{0:T(1024)(128)(2,1)}, u32[]{:S(2)}) copy-start(bf16[2048]{0:T(1024)(128)(2,1)} %param.17) | copy-start | bytes 12292
  69.2 50.9 %copy-start.9 = (s32[4]{0:T(128)S(1)}, s32[4]{0:T(128)}, u32[]{:S(2)}) copy-start(s32[4]{0:T(128)} %param.21) | copy-start | bytes 52
  119.2 416.6 %all-gather.17.cloned.1.call-start = ((), (), s32[]{:S(2)}) async-start(), calls=%async_computation.6 | async-start | bytes 35651584 | tf_op jit(solution)/shard_map/all_gather | solution.py:135
  119.8 487.3 %reduce-scatter.2.cloned.1.call-start = ((), (), s32[]{:S(2)}) async-start(), calls=%async_computation.7 | async-start | bytes 6291456 | tf_op jit(solution)/shard_map/reduce_scatter | solution.py:138
  309.9 1.6 copy-start.3
  309.9 2.2 copy-start.4
  385.7 15.3 %copy-start.2 = (bf16[4096,256]{1,0:T(8,128)(2,1)S(1)}, bf16[4096,256]{1,0:T(8,128)(2,1)}, u32[]{:S(2)}) copy-start(bf16[4096,256]{1,0:T(8,128)(2,1)} %get-tuple-element.452) | copy-start | bytes 6291460 | tf_op jit(solution)/shard_map/while
  437.3 15.6 %copy-start.2 = (bf16[4096,256]{1,0:T(8,128)(2,1)S(1)}, bf16[4096,256]{1,0:T(8,128)(2,1)}, u32[]{:S(2)}) copy-start(bf16[4096,256]{1,0:T(8,128)(2,1)} %get-tuple-element.452) | copy-start | bytes 6291460 | tf_op jit(solution)/shard_map/while
  552.6 59.3 %copy-start.1 = (bf16[512,512]{1,0:T(8,128)(2,1)S(1)}, bf16[512,512]{1,0:T(8,128)(2,1)}, u32[]{:S(2)}) copy-start(bf16[512,512]{1,0:T(8,128)(2,1)} %param.15) | copy-start | bytes 1572868
Sparse Core Ops, SparseCore 0:
  9.5 53.1 all-gather.6
  64.8 48.8 all-gather.12
  115.4 166.5 all-gather.10
  284.0 41.0 all-gather.8
  327.1 40.5 all-gather.14
  369.1 166.7 all-gather.16
  552.8 54.3 reduce-scatter.1
where the time goes:
time: 619 us
  waiting for transfers between devices  423 us (68%)
  matrix products  109 us (18%)
  other arithmetic  50.7 us (8%)
  local copies, waits for them, and re-layouts  21.9 us (4%)
  between operations  13.7 us (2%)
    all_gather x1, waiting for transfers between devices, shards(): lax.all_gather(w_query, 'fsdp', axis=0, tiled=True)  162 us
    all_gather x1, waiting for transfers between devices, shards(): lax.all_gather(w_out, 'fsdp', axis=1, tiled=True)  59.9 us
    reduce_scatter x1, waiting for transfers between devices, shards(): lax.psum_scatter(terms.astype(jnp.bfloat16), 'tp', scatter_dimension=0, t...  54.5 us
    all_gather x1, waiting for transfers between devices, shards(): lax.all_gather(key_part, 'fsdp', axis=0, tiled=True)  45.9 us
    all_gather x1, waiting for transfers between devices, shards(): lax.all_gather(value_part, 'fsdp', axis=0, tiled=True)  44.6 us
    all_gather x1, waiting for transfers between devices, shards(): value_piece = lax.all_gather(values, 'fsdp', axis=0, tiled=True)  42.6 us
    dot_general x2, matrix products, fold_block(): jnp.einsum('kgqn,nkd->kgqd', weights.astype(jnp.bfloat16), value_block, p...  35.9 us
    reduce_sum x2, other arithmetic, fold_block(): total = total * factor + jnp.sum(weights, axis=3)  30.9 us
  transfers between devices with their start and end apart: 7, of which 7 were waited for; matrix products, arithmetic and copies ran while one was open for 25% of the time, Pallas kernels for 0%

commit v1 on v0

v1 whole, which is shorter than its diff:
```python
import functools
import math

import jax
import jax.numpy as jnp
from jax import lax
from jax.experimental import pallas as pl
from jax.experimental.pallas import tpu as pltpu
from jax.sharding import PartitionSpec as P

HEAD = 128
QHEADS = 32
KVHEADS = 4

ROPE_BASE = 1000000.0
EPSILON = 1e-06
FLOOR = -1e30
MESH = pl.DeviceIdType.MESH
PARTS = 2


def token_layout(seq_lengths, token_index):
    seq_ends = jnp.cumsum(seq_lengths)
    seq_starts = seq_ends - seq_lengths
    member = (token_index[:, None] >= seq_ends[None, :]).astype(jnp.int32)
    segment = jnp.sum(member, axis=1)
    one_hot = segment[:, None] == jnp.arange(seq_lengths.shape[0], dtype=jnp.int32)[None, :]
    return jnp.sum(jnp.where(one_hot, seq_starts[None, :], 0), axis=1)


def rotary_tables(position):
    half_size = HEAD // 2
    frequency = jnp.exp(
        jnp.arange(half_size, dtype=jnp.float32) * (-2.0 * math.log(ROPE_BASE) / HEAD)
    )
    angle = position.astype(jnp.float32)[:, None] * frequency[None, :]
    cos, sin = jnp.cos(angle), jnp.sin(angle)
    return jnp.concatenate([cos, cos], axis=1), jnp.concatenate([-sin, sin], axis=1)


def gather_kernel(n, block_ref, out_ref, local_sem, send_sem, pass_sem, recv_sem):
    me = lax.axis_index("fsdp")
    partner = me + 1 - 2 * lax.rem(me, 2)
    half = n // 2
    barrier = pltpu.get_barrier_semaphore()
    for d in range(1, half):
        pl.semaphore_signal(
            barrier, inc=1, device_id={"fsdp": lax.rem(me + 2 * d, n)}, device_id_type=MESH
        )
    pl.semaphore_signal(barrier, inc=1, device_id={"fsdp": partner}, device_id_type=MESH)
    pl.semaphore_wait(barrier, half)

    def first(d, target):
        return pltpu.make_async_remote_copy(
            src_ref=block_ref,
            dst_ref=out_ref.at[me],
            send_sem=send_sem.at[d],
            recv_sem=recv_sem.at[me],
            device_id={"fsdp": target},
            device_id_type=MESH,
        )

    def onward(d, source):
        return pltpu.make_async_remote_copy(
            src_ref=out_ref.at[source],
            dst_ref=out_ref.at[source],
            send_sem=pass_sem.at[d],
            recv_sem=recv_sem.at[source],
            device_id={"fsdp": partner},
            device_id_type=MESH,
        )

    own = pltpu.make_async_copy(block_ref, out_ref.at[me], local_sem)
    own.start()
    sends = [first(d, lax.rem(me + 2 * d, n)) for d in range(1, half)] + [first(0, partner)]
    for copy in sends:
        copy.start()
    passes = []
    for d in range(1, half):
        copy = onward(d, lax.rem(me - 2 * d + n, n))
        copy.wait_recv()
        copy.start()
        passes.append(copy)
    onward(0, partner).wait_recv()
    for d in range(1, half):
        onward(d, lax.rem(partner - 2 * d + n, n)).wait_recv()
    for copy in sends + passes:
        copy.wait_send()
    own.wait()


def gather_blocks(block, n):
    rows, cols = block.shape
    if n % 2:
        return lax.all_gather(block, "fsdp", axis=0, tiled=True)
    out = pl.pallas_call(
        functools.partial(gather_kernel, n),
        out_shape=jax.ShapeDtypeStruct((n, rows, cols), block.dtype),
        in_specs=[pl.BlockSpec(memory_space=pltpu.VMEM)],
        out_specs=pl.BlockSpec(memory_space=pltpu.VMEM),
        scratch_shapes=[
            pltpu.SemaphoreType.DMA,
            pltpu.SemaphoreType.DMA((n // 2,)),
            pltpu.SemaphoreType.DMA((n // 2,)),
            pltpu.SemaphoreType.DMA((n,)),
        ],
        compiler_params=pltpu.CompilerParams(collective_id=0, has_side_effects=True),
        cost_estimate=pl.CostEstimate(
            flops=0, bytes_accessed=100_000_000, transcendentals=0
        ),
        name="kv_gather",
    )(block)
    return out.reshape(n * rows, cols)


def attend_kernel(
    block, reach_ref, query_ref, cos_ref, sin_ref, begin_ref, index_ref, key_ref, value_ref, out_ref
):
    query = query_ref[...]
    query = query * cos_ref[...] + pltpu.roll(query, HEAD // 2, 1) * sin_ref[...]
    query = query.astype(jnp.bfloat16)
    rows = query.shape[0]
    begin, index = begin_ref[...], index_ref[...]
    lowest, top = reach_ref[0], reach_ref[1]
    factor = HEAD ** (-0.5) * math.log2(math.e)

    def step(i, carried):
        running, total, summed = carried
        offset = pl.multiple_of((top - i) * block, block)
        scores = lax.dot_general(
            query,
            key_ref[pl.ds(offset, block), :],
            (((1,), (1,)), ((), ())),
            preferred_element_type=jnp.float32,
        )
        place = offset + lax.broadcasted_iota(jnp.int32, (rows, block), 1)
        scores = jnp.where((place >= begin) & (place <= index), scores * factor, FLOOR)
        highest = jnp.maximum(running, jnp.max(scores, axis=1, keepdims=True))
        weights = jnp.exp2(scores - highest)
        shrink = jnp.exp2(running - highest)
        total = total * shrink + jnp.sum(weights, axis=1, keepdims=True)
        update = jnp.dot(
            weights.astype(jnp.bfloat16),
            value_ref[pl.ds(offset, block), :],
            preferred_element_type=jnp.float32,
        )
        return highest, total, summed * shrink + update

    start = (
        jnp.full((rows, 1), FLOOR, jnp.float32),
        jnp.zeros((rows, 1), jnp.float32),
        jnp.zeros((rows, HEAD), jnp.float32),
    )
    running, total, summed = lax.fori_loop(0, top - lowest + 1, step, start)
    out_ref[...] = (summed / total).astype(jnp.bfloat16)


def attend(query, cos, sin, begin, index, pairs, heads, local_kv):
    rows, tokens = query.shape[0], pairs.shape[0]
    block = 2 * rows if tokens % (2 * rows) == 0 else rows
    reach = jnp.stack([begin[0] // block, index[0] // block]).astype(jnp.int32)
    per_kv = heads // local_kv
    whole = lambda width: pl.BlockSpec((rows, width), lambda h: (0, 0))
    return pl.pallas_call(
        functools.partial(attend_kernel, block),
        grid=(heads,),
        out_shape=jax.ShapeDtypeStruct((rows, heads * HEAD), jnp.bfloat16),
        in_specs=[
            pl.BlockSpec(memory_space=pltpu.SMEM),
            pl.BlockSpec((rows, HEAD), lambda h: (0, h)),
            whole(HEAD),
            whole(HEAD),
            whole(1),
            whole(1),
            pl.BlockSpec((tokens, HEAD), lambda h: (0, h // per_kv)),
            pl.BlockSpec((tokens, HEAD), lambda h: (0, local_kv + h // per_kv)),
        ],
        out_specs=pl.BlockSpec((rows, HEAD), lambda h: (0, h)),
        compiler_params=pltpu.CompilerParams(vmem_limit_bytes=24 * 1024 * 1024),
        cost_estimate=pl.CostEstimate(
            flops=4 * rows * tokens * heads * HEAD,
            bytes_accessed=100_000_000,
            transcendentals=rows * tokens * heads,
        ),
        name="attend",
    )(reach, query, cos, sin, begin[:, None], index[:, None], pairs, pairs)


def finish_kernel(parts, others, own_ref, *refs):
    width = own_ref.shape[1] // parts
    out_ref = refs[-1]
    for part in range(parts):
        cut = slice(part * width, (part + 1) * width)
        total = own_ref[:, cut].astype(jnp.float32)
        for term in refs[part * (others + 1) : (part + 1) * (others + 1)]:
            total = total + term[...].astype(jnp.float32)
        out_ref[:, cut] = total


def finish(own_rows, terms, n):
    rows, cols = own_rows.shape
    parts = len(terms)
    wide, narrow = cols // n, cols // n // parts
    return pl.pallas_call(
        functools.partial(finish_kernel, parts, len(terms[0]) - 1),
        grid=(n,),
        out_shape=jax.ShapeDtypeStruct((rows, cols), jnp.float32),
        in_specs=[pl.BlockSpec((rows, wide), lambda f: (0, f))]
        + [pl.BlockSpec((rows, narrow), lambda f: (0, f))] * sum(len(t) for t in terms),
        out_specs=pl.BlockSpec((rows, wide), lambda f: (0, f)),
        compiler_params=pltpu.CompilerParams(vmem_limit_bytes=16 * 1024 * 1024),
        name="finish",
    )(own_rows, *[term for some in terms for term in some])


def shards(
    hidden, norm_gain, w_query, w_key, w_value, bias_query, bias_key, bias_value, w_out, seq_lengths
):
    n, tp = lax.axis_size("fsdp"), lax.axis_size("tp")
    tok_rows = hidden.shape[0]
    query_cols = w_query.shape[1]
    local_heads = query_cols // HEAD
    group_size = QHEADS // KVHEADS
    local_kv = max(local_heads // group_size, 1)
    first_kv = lax.axis_index("tp") * local_heads // group_size
    key_cols = local_kv * HEAD
    key_part = lax.dynamic_slice_in_dim(w_key, first_kv * HEAD, key_cols, 1)
    value_part = lax.dynamic_slice_in_dim(w_value, first_kv * HEAD, key_cols, 1)
    key_bias = lax.dynamic_slice_in_dim(bias_key, first_kv * HEAD, key_cols, 0)
    value_bias = lax.dynamic_slice_in_dim(bias_value, first_kv * HEAD, key_cols, 0)
    weights = lax.all_gather(
        jnp.concatenate([key_part, value_part, w_query], axis=1), "fsdp", axis=0, tiled=True
    )

    local_index = lax.axis_index("fsdp") * tok_rows + jnp.arange(tok_rows, dtype=jnp.int32)
    begin = token_layout(seq_lengths, local_index)
    cos, sin = rotary_tables(local_index - begin)
    widened = hidden.astype(jnp.float32)
    scale = lax.rsqrt(jnp.mean(widened * widened, axis=1, keepdims=True) + EPSILON)
    normed = (widened * scale * norm_gain[None, :]).astype(jnp.bfloat16)

    part_cols = w_out.shape[1] // PARTS
    own_parts = [w_out[:, part * part_cols : (part + 1) * part_cols] for part in range(PARTS)]
    weights, own_parts = lax.optimization_barrier((weights, own_parts))
    out_parts = [lax.all_gather(part, "fsdp", axis=1, tiled=True) for part in own_parts]

    pairs = jnp.dot(normed, weights[:, : 2 * key_cols], preferred_element_type=jnp.float32)
    pairs = pairs + jnp.concatenate([key_bias, value_bias]).astype(jnp.float32)[None, :]
    pieces = []
    for head in range(local_kv):
        one = pairs[:, head * HEAD : (head + 1) * HEAD]
        turned = jnp.concatenate([one[:, HEAD // 2 :], one[:, : HEAD // 2]], axis=1)
        pieces.append(one * cos + turned * sin)
    pieces.append(pairs[:, key_cols:])
    block = jnp.concatenate(pieces, axis=1).astype(jnp.bfloat16)
    query = jnp.dot(normed, weights[:, 2 * key_cols :], preferred_element_type=jnp.float32)
    query = query + bias_query.astype(jnp.float32)[None, :]
    gathered = gather_blocks(block, n)
    attended = attend(query, cos, sin, begin, local_index, gathered, local_heads, local_kv)

    share = tok_rows // tp
    me = lax.axis_index("tp")
    own_rows = lax.dynamic_slice_in_dim(hidden, me * share, share, 0)
    own_attended = lax.dynamic_slice_in_dim(attended, me * share, share, 0)
    terms = []
    for part in range(PARTS):
        some = []
        for d in range(1, tp):
            peer = lax.rem(me + d, tp)
            rows = lax.dynamic_slice_in_dim(attended, peer * share, share, 0)
            term = jnp.dot(rows, out_parts[part], preferred_element_type=jnp.float32)
            some.append(
                lax.ppermute(
                    term.astype(jnp.bfloat16), "tp", [(i, (i + d) % tp) for i in range(tp)]
                )
            )
        some.append(jnp.dot(own_attended, out_parts[part], preferred_element_type=jnp.float32))
        terms.append(some)
    return finish(own_rows, terms, n)


def solution(mesh):
    in_specs = (
        P("fsdp", None),
        P(),
        P("fsdp", "tp"),
        P("fsdp", None),
        P("fsdp", None),
        P("tp"),
        P(),
        P(),
        P("tp", "fsdp"),
        P(),
    )
    out_specs = P(("fsdp", "tp"), None)
    return jax.shard_map(shards, mesh=mesh, in_specs=in_specs, out_specs=out_specs, check_vma=False)
```

time: 619 us -> 573 us (0.926)
  Pallas kernels: 0 us -> 83.9 us
  matrix products: 109 us -> 51.4 us
  other arithmetic: 50.7 us -> 9.53 us
  waiting for transfers between devices: 423 us -> 396 us
  local copies, waits for them, and re-layouts: 21.9 us -> 9.9 us
    pallas_call x0 -> x3, Pallas kernels: none -> 83.9 us  [the longest x1 60 us: gather_blocks(): pl.pallas_call(functools.partial(gather_kernel, n), out_shape=jax.ShapeDt...]
    dot_general x8 -> x6, matrix products: 109 us -> 51.4 us  [the longest x1 17.4 us: shards(): jnp.dot(normed, weights[:, 2 * key_cols:], preferred_element_type=jnp.flo...]
    reduce_scatter x1 -> x0, waiting for transfers between devices: 54.5 us -> none  [shards(): lax.psum_scatter(terms.astype(jnp.bfloat16), 'tp', scatter_dimension=0, t...]
    reduce_sum x3 -> x1, other arithmetic: 31 us -> 0.09 us  [token_layout(): return jnp.sum(jnp.where(one_hot, seq_starts[None, :], 0), axis=1)]
    all_gather x6 -> x3, waiting for transfers between devices: 367 us -> 383 us  [the longest x1 209 us: shards(): lax.all_gather(jnp.concatenate([key_part, value_part, w_query], axis=1),...]
    ppermute x0 -> x2, waiting for transfers between devices: none -> 12.6 us  [shards(): lax.ppermute(term.astype(jnp.bfloat16), 'tp', [(i, (i + d) % tp) for i in...]
    concatenate x4 -> x0, local copies, waits for them, and re-layouts: 6.58 us -> none  [the longest x2 6.39 us: rotary(): jnp.concatenate([-vectors[..., half_size:], vectors[..., :half_size]], ax...]
  transfers between devices with their start and end apart: 7 -> 5, of which waited for: 7 -> 4; matrix products, arithmetic and copies ran while one was open for 25% -> 11% of each run, Pallas kernels for 0% -> 13%
where the time goes in v1:
time: 573 us; the launch traced here: 572 us
  waiting for transfers between devices  396 us (69%)
  Pallas kernels  83.9 us (15%)
  matrix products  51.4 us (9%)
  between operations  18.2 us (3%)
  local copies, waits for them, and re-layouts  9.9 us (2%)
  other arithmetic  9.53 us (2%)
    all_gather x1, waiting for transfers between devices, shards(): lax.all_gather(jnp.concatenate([key_part, value_part, w_query], axis=1),...  209 us
    all_gather x2, waiting for transfers between devices, shards(): lax.all_gather(part, 'fsdp', axis=1, tiled=True)  174 us
    pallas_call x1, Pallas kernels, gather_blocks(): pl.pallas_call(functools.partial(gather_kernel, n), out_shape=jax.ShapeDt...  60 us
    dot_general x1, matrix products, shards(): jnp.dot(normed, weights[:, 2 * key_cols:], preferred_element_type=jnp.flo...  17.4 us
    dot_general x2, matrix products, shards(): term = jnp.dot(rows, out_parts[part], preferred_element_type=jnp.float32)  17.3 us
    pallas_call x1, Pallas kernels, attend(): pl.pallas_call(functools.partial(attend_kernel, block), grid=(heads,), ou...  14.2 us
    ppermute x2, waiting for transfers between devices, shards(): lax.ppermute(term.astype(jnp.bfloat16), 'tp', [(i, (i + d) % tp) for i in...  12.6 us
  transfers between devices with their start and end apart: 5, of which 4 were waited for; matrix products, arithmetic and copies ran while one was open for 11% of the time, Pallas kernels for 13%

profile of v1, /device:TPU:0, one launch (start us, length us, event | category | flops | bytes accessed | tf_op | source)
XLA Modules:
  0.0 572.2 jit_solution(18227206059705770313)
XLA Ops:
  6.5 0.0 all-gather.4.cloned.1.call-start
  6.5 1.2 constant_dynamic-slice_fusion
  7.8 3.3 pad_maximum_fusion
  11.0 0.0 all-gather.4.cloned.1.call-update
  11.0 0.0 all-gather.8.cloned.1.call-start
  11.1 1.5 fusion.30
  12.6 208.8 %all-gather.4.cloned.1.call-done = bf16[8192,2560]{1,0:T(8,128)(2,1)} async-done(((bf16[512,2560]{1,0:T(8,128)(2,1)}), bf16[8192,2560]{1,0:T(8,128)(2,1)}) %all-gather.4.cloned.1.call-update) | async-done | bytes 41943056 | tf_op jit(solution)/shard_map/all_gather | solution.py:231
  221.5 0.0 all-gather.8.cloned.1.call-update
  221.5 0.0 copy-start.7
  221.5 0.0 all-gather.6.cloned.1.call-start
  221.6 0.7 all-gather.6.cloned.1.call-update
  222.3 0.2 reduce-window.8
  222.4 0.1 convert_reduce_fusion
  222.5 0.1 select_reduce_fusion
  222.6 0.5 slice.44
  224.8 0.5 slice.45
  228.5 0.1 dynamic_slice.25
  228.6 0.1 dynamic_slice.26
  228.7 0.1 copy.12.begin_ref
  228.8 0.0 copy-start.4
  228.9 0.1 pad_add_fusion.reach_ref
  229.0 3.5 fusion.2
  232.5 0.5 fusion.25
  233.1 0.0 copy-done.4
  233.1 0.1 constant_dynamic-slice_fusion.2.own_ref
  233.3 6.1 %fusion.10 = f32[256,512]{1,0:T(8,128)S(1)} fusion(bf16[8192,2560]{1,0:T(8,128)(2,1)} %all-gather.4.cloned.1.call-done, bf16[256,8192]{1,0:T(8,128)(2,1)S(1)} %copy-done.4, f32[8192]{0:T(1024)S(1)} %copy-done.7, f32[256]{0:T(256)S(1)} %add_rsqrt_fusion, f32[512]{0:T(512)S(1)} %maximum_convert_fusion), kind=kOutput, calls=%fused_computation.13 | convolution fusion | flops 2156003328 | bytes 13143040 | tf_op jit(solution)/shard_map/dot_general | solution.py:247
  239.4 0.1 fusion.31
  239.5 0.2 fusion.24
  239.7 0.8 fusion.22
  240.5 0.7 pad_maximum_fusion.1.block_ref
  241.2 60.0 %kv_gather.1 = bf16[16,256,512]{2,1,0:T(8,128)(2,1)} custom-call(bf16[256,512]{1,0:T(8,128)(2,1)} %pad_maximum_fusion.1.block_ref), custom_call_target="tpu_custom_call" | custom-call | bytes 100000000 | tf_op jit(solution)/shard_map/kv_gather/pallas_call | solution.py:96
  301.2 17.4 %fusion.7.query_ref = f32[256,2048]{1,0:T(8,128)} fusion(bf16[8192,2560]{1,0:T(8,128)(2,1)} %all-gather.4.cloned.1.call-done, bf16[256,8192]{1,0:T(8,128)(2,1)} %param.10, f32[8192]{0:T(1024)S(1)} %copy-done.7, f32[256]{0:T(256)S(1)} %add_rsqrt_fusion, f32[2048]{0:T(1024)S(1)} %convert_element_type.36), kind=kOutput, calls=%fused_computation.11 | convolution fusion | flops 8598847488 | bytes 39887872 | tf_op jit(solution)/shard_map/dot_general | solution.py:256
  318.6 2.3 copy-done
  320.9 0.9 copy-done.1
  321.8 1.6 copy-done.2
  323.5 14.2 %attend.1 = bf16[256,2048]{1,0:T(8,128)(2,1)S(1)} custom-call(s32[2]{0:T(128)S(1)} %pad_add_fusion.reach_ref, f32[256,2048]{1,0:T(8,128)S(1)} %copy-done.2, f32[256,128]{1,0:T(8,128)S(1)} %copy-done.1, f32[256,128]{1,0:T(8,128)S(1)} %get-tuple-element.12.sin_ref, s32[256,1]{1,0:T(8,128)S(1)} %copy.12.begin_ref, s32[256,1]{1,0:T(8,128)S(1)} %iota_add_fusion.index_ref, ...), custom_call_target="tpu_custom_call" | custom-call | flops 8589934592 | bytes 100000000 | tf_op jit(solution)/shard_map/attend/pallas_call | solution.py:164
  337.7 54.4 %all-gather.8.cloned.1.call-done = bf16[2048,4096]{1,0:T(8,128)(2,1)} async-done(((bf16[2048,256]{1,0:T(8,128)(2,1)}), bf16[2048,4096]{1,0:T(8,128)(2,1)}) %all-gather.8.cloned.1.call-update) | async-done | bytes 16777232 | tf_op jit(solution)/shard_map/all_gather | solution.py:245
  392.1 9.1 %convolution_convert_fusion = bf16[128,4096]{1,0:T(8,128)(2,1)} fusion(bf16[2048,4096]{1,0:T(8,128)(2,1)} %all-gather.8.cloned.1.call-done, bf16[256,2048]{1,0:T(8,128)(2,1)S(1)} %attend.1, s32[]{:T(128)S(6)} %select_n.35), kind=kOutput, calls=%fused_computation.9 | convolution fusion | flops 2148007936 | bytes 18350084 | tf_op jit(solution)/shard_map/dot_general | solution.py:271
  401.2 1.5 collective-permute-start.1
  402.7 119.7 %all-gather.6.cloned.1.call-done = bf16[2048,4096]{1,0:T(8,128)(2,1)} async-done(((bf16[2048,256]{1,0:T(8,128)(2,1)}), bf16[2048,4096]{1,0:T(8,128)(2,1)}) %all-gather.6.cloned.1.call-update) | async-done | bytes 16777232 | tf_op jit(solution)/shard_map/all_gather | solution.py:245
  522.4 8.3 %convolution_convert_fusion.1 = bf16[128,4096]{1,0:T(8,128)(2,1)S(1)} fusion(bf16[2048,4096]{1,0:T(8,128)(2,1)} %all-gather.6.cloned.1.call-done, bf16[256,2048]{1,0:T(8,128)(2,1)S(1)} %attend.1, s32[]{:T(128)S(6)} %select_n.35), kind=kOutput, calls=%fused_computation.10 | convolution fusion | flops 2148007936 | bytes 18350084 | tf_op jit(solution)/shard_map/dot_general | solution.py:271
  530.6 1.6 collective-permute-start
  532.2 0.7 copy-done.3
  532.9 2.4 fusion.15.refs_3_
  535.3 8.1 %fusion.17.refs_1_ = f32[128,4096]{1,0:T(8,128)S(1)} fusion(bf16[2048,4096]{1,0:T(8,128)(2,1)} %all-gather.6.cloned.1.call-done, bf16[256,2048]{1,0:T(8,128)(2,1)S(1)} %attend.1, s32[]{:T(128)S(6)} %select_n.29), kind=kOutput, calls=%fused_computation.16 | convolution fusion | flops 2147483648 | bytes 19398660 | tf_op jit(solution)/shard_map/dot_general | solution.py:277
  543.4 0.0 collective-permute-done.1.refs_2_
  543.4 12.6 %collective-permute-done.refs_0_ = bf16[128,4096]{1,0:T(8,128)(2,1)S(1)} collective-permute-done((bf16[128,4096]{1,0:T(8,128)(2,1)S(1)}, bf16[128,4096]{1,0:T(8,128)(2,1)S(1)}, u32[]{:S(2)}, u32[]{:S(2)}) %collective-permute-start) | collective-permute-done | bytes 1048608 | tf_op jit(solution)/shard_map/ppermute | solution.py:273
  556.0 9.7 %finish.1 = f32[128,8192]{1,0:T(8,128)} custom-call(bf16[128,8192]{1,0:T(8,128)(2,1)S(1)} %constant_dynamic-slice_fusion.2.own_ref, bf16[128,4096]{1,0:T(8,128)(2,1)S(1)} %collective-permute-done.refs_0_, f32[128,4096]{1,0:T(8,128)S(1)} %fusion.17.refs_1_, bf16[128,4096]{1,0:T(8,128)(2,1)} %collective-permute-done.1.refs_2_, f32[128,4096]{1,0:T(8,128)S(1)} %fusion.15.refs_3_), custom_call_target="tpu_custom_call" | custom-call | tf_op jit(solution)/shard_map/finish/pallas_call | solution.py:204
  (24 shorter events, 0.1 us)
Async XLA Ops:
  6.5 4.6 copy-start.5
  6.5 214.9 %all-gather.4.cloned.1.call-start = ((), (), s32[]{:S(2)}) async-start(), calls=%async_computation | async-start | bytes 44564480 | tf_op jit(solution)/shard_map/all_gather | solution.py:231
  11.0 211.2 %copy-start.10 = (s32[4]{0:T(128)S(1)}, s32[4]{0:T(128)}, u32[]{:S(2)}) copy-start(s32[4]{0:T(128)} %param.19) | copy-start | bytes 52
  11.0 217.5 %copy-start.8 = (bf16[512]{0:T(512)(128)(2,1)S(1)}, bf16[512]{0:T(512)(128)(2,1)}, u32[]{:S(2)}) copy-start(bf16[512]{0:T(512)(128)(2,1)} %param.16) | copy-start | bytes 3076
  11.0 217.6 %copy-start.9 = (bf16[512]{0:T(512)(128)(2,1)S(1)}, bf16[512]{0:T(512)(128)(2,1)}, u32[]{:S(2)}) copy-start(bf16[512]{0:T(512)(128)(2,1)} %param.17) | copy-start | bytes 3076
  11.0 217.7 %copy-start.6 = (bf16[2048]{0:T(1024)(128)(2,1)S(1)}, bf16[2048]{0:T(1024)(128)(2,1)}, u32[]{:S(2)}) copy-start(bf16[2048]{0:T(1024)(128)(2,1)} %param.15) | copy-start | bytes 12292
  11.0 381.0 %all-gather.8.cloned.1.call-start = ((), (), s32[]{:S(2)}) async-start(), calls=%async_computation.2 | async-start | bytes 17825792 | tf_op jit(solution)/shard_map/all_gather | solution.py:245
  221.5 11.8 %copy-start.7 = (f32[8192]{0:T(1024)S(1)}, f32[8192]{0:T(1024)}, u32[]{:S(2)}) copy-start(f32[8192]{0:T(1024)} %param.11) | copy-start | bytes 98308
  221.5 300.8 %all-gather.6.cloned.1.call-start = ((), (), s32[]{:S(2)}) async-start(), calls=%async_computation.1 | async-start | bytes 17825792 | tf_op jit(solution)/shard_map/all_gather | solution.py:245
  228.8 4.2 copy-start.4
  318.6 2.3 copy-start
  320.9 0.9 copy-start.1
  321.8 1.6 copy-start.2
  401.2 142.3 %collective-permute-start.1 = (bf16[128,4096]{1,0:T(8,128)(2,1)}, bf16[128,4096]{1,0:T(8,128)(2,1)}, u32[]{:S(2)}, u32[]{:S(2)}) collective-permute-start(bf16[128,4096]{1,0:T(8,128)(2,1)} %convolution_convert_fusion), channel_id=1, source_target_pairs={{0,1},{1,0},{2,3},{3,2},{4,5},{5,4},{6,7},{7,6},{8,9},{9,8},{10,11... | collective-permute-start | bytes 3145736 | tf_op jit(solution)/shard_map/ppermute | solution.py:273
  522.4 10.5 %copy-start.3 = (bf16[2048,4096]{1,0:T(8,128)(2,1)S(1)}, bf16[2048,4096]{1,0:T(8,128)(2,1)}, u32[]{:S(2)}) copy-start(bf16[2048,4096]{1,0:T(8,128)(2,1)} %all-gather.8.cloned.1.call-done) | copy-start | bytes 50331652
  530.6 25.4 %collective-permute-start = (bf16[128,4096]{1,0:T(8,128)(2,1)S(1)}, bf16[128,4096]{1,0:T(8,128)(2,1)S(1)}, u32[]{:S(2)}, u32[]{:S(2)}) collective-permute-start(bf16[128,4096]{1,0:T(8,128)(2,1)S(1)} %convolution_convert_fusion.1), channel_id=1, source_target_pairs={{0,1},{1,0},{2,3},{3,2},{4,5},{5,4},{6,7},{7,6},{8,9},{9,8},{10,11... | collective-permute-start | bytes 3145736 | tf_op jit(solution)/shard_map/ppermute | solution.py:273
Sparse Core Ops, SparseCore 0:
  11.2 210.2 all-gather.3
  223.6 168.3 all-gather.7
  394.2 128.0 all-gather.5

commit v2 on v1

--- a/solution.py
+++ b/solution.py
@@ -16,7 +16,7 @@
 EPSILON = 1e-06
 FLOOR = -1e30
 MESH = pl.DeviceIdType.MESH
-PARTS = 2
+CHUNKS = 4
 
 
 def token_layout(seq_lengths, token_index):
@@ -38,60 +38,67 @@
     return jnp.concatenate([cos, cos], axis=1), jnp.concatenate([-sin, sin], axis=1)
 
 
-def gather_kernel(n, block_ref, out_ref, local_sem, send_sem, pass_sem, recv_sem):
+def gather_kernel(n, block_ref, out_ref, local_sem, send_sem, recv_sem):
     me = lax.axis_index("fsdp")
-    partner = me + 1 - 2 * lax.rem(me, 2)
-    half = n // 2
+    steps = n // 4
+    beside = me + 2 - 4 * lax.rem(lax.div(me, 2), 2)
+    turn = 1 - 2 * lax.rem(me, 2)
+    partner = me + turn
     barrier = pltpu.get_barrier_semaphore()
-    for d in range(1, half):
-        pl.semaphore_signal(
-            barrier, inc=1, device_id={"fsdp": lax.rem(me + 2 * d, n)}, device_id_type=MESH
-        )
-    pl.semaphore_signal(barrier, inc=1, device_id={"fsdp": partner}, device_id_type=MESH)
-    pl.semaphore_wait(barrier, half)
-
-    def first(d, target):
-        return pltpu.make_async_remote_copy(
-            src_ref=block_ref,
-            dst_ref=out_ref.at[me],
-            send_sem=send_sem.at[d],
-            recv_sem=recv_sem.at[me],
+    for target in [lax.rem(me + 4 * d, n) for d in range(1, steps)] + [beside, partner]:
+        pl.semaphore_signal(barrier, inc=1, device_id={"fsdp": target}, device_id_type=MESH)
+    pl.semaphore_wait(barrier, steps + 1)
+
+    started = []
+
+    def send(source_ref, source, target):
+        copy = pltpu.make_async_remote_copy(
+            src_ref=source_ref,
+            dst_ref=out_ref.at[source],
+            send_sem=send_sem.at[len(started)],
+            recv_sem=recv_sem.at[source],
             device_id={"fsdp": target},
             device_id_type=MESH,
         )
-
-    def onward(d, source):
-        return pltpu.make_async_remote_copy(
-            src_ref=out_ref.at[source],
+        copy.start()
+        started.append(copy)
+
+    def arrived(source):
+        pltpu.make_async_remote_copy(
+            src_ref=block_ref,
             dst_ref=out_ref.at[source],
-            send_sem=pass_sem.at[d],
+            send_sem=send_sem.at[0],
             recv_sem=recv_sem.at[source],
             device_id={"fsdp": partner},
             device_id_type=MESH,
-        )
+        ).wait_recv()
 
     own = pltpu.make_async_copy(block_ref, out_ref.at[me], local_sem)
     own.start()
-    sends = [first(d, lax.rem(me + 2 * d, n)) for d in range(1, half)] + [first(0, partner)]
-    for copy in sends:
-        copy.start()
-    passes = []
-    for d in range(1, half):
-        copy = onward(d, lax.rem(me - 2 * d + n, n))
-        copy.wait_recv()
-        copy.start()
-        passes.append(copy)
-    onward(0, partner).wait_recv()
-    for d in range(1, half):
-        onward(d, lax.rem(partner - 2 * d + n, n)).wait_recv()
-    for copy in sends + passes:
+    for d in range(1, steps):
+        send(block_ref, me, lax.rem(me + 4 * d, n))
+    send(block_ref, me, beside)
+    send(block_ref, me, partner)
+    for d in range(1, steps):
+        source = lax.rem(me - 4 * d + n, n)
+        arrived(source)
+        send(out_ref.at[source], source, beside)
+        send(out_ref.at[source], source, partner)
+    for d in range(steps):
+        source = lax.rem(beside - 4 * d + n, n)
+        arrived(source)
+        send(out_ref.at[source], source, partner)
+    for first in (partner, beside + turn):
+        for d in range(steps):
+            arrived(lax.rem(first - 4 * d + n, n))
+    for copy in started:
         copy.wait_send()
     own.wait()
 
 
 def gather_blocks(block, n):
     rows, cols = block.shape
-    if n % 2:
+    if n % 4:
         return lax.all_gather(block, "fsdp", axis=0, tiled=True)
     out = pl.pallas_call(
         functools.partial(gather_kernel, n),
@@ -100,8 +107,7 @@
         out_specs=pl.BlockSpec(memory_space=pltpu.VMEM),
         scratch_shapes=[
             pltpu.SemaphoreType.DMA,
-            pltpu.SemaphoreType.DMA((n // 2,)),
-            pltpu.SemaphoreType.DMA((n // 2,)),
+            pltpu.SemaphoreType.DMA((n,)),
             pltpu.SemaphoreType.DMA((n,)),
         ],
         compiler_params=pltpu.CompilerParams(collective_id=0, has_side_effects=True),
@@ -186,31 +192,31 @@
     )(reach, query, cos, sin, begin[:, None], index[:, None], pairs, pairs)
 
 
-def finish_kernel(parts, others, own_ref, *refs):
-    width = own_ref.shape[1] // parts
+def finish_kernel(base_ref, *refs):
     out_ref = refs[-1]
-    for part in range(parts):
-        cut = slice(part * width, (part + 1) * width)
-        total = own_ref[:, cut].astype(jnp.float32)
-        for term in refs[part * (others + 1) : (part + 1) * (others + 1)]:
+    width = refs[0].shape[1]
+    chunks = base_ref.shape[1] // width
+    for chunk in range(chunks):
+        cut = slice(chunk * width, (chunk + 1) * width)
+        total = base_ref[:, cut]
+        for term in refs[chunk:-1:chunks]:
             total = total + term[...].astype(jnp.float32)
         out_ref[:, cut] = total
 
 
-def finish(own_rows, terms, n):
-    rows, cols = own_rows.shape
-    parts = len(terms)
-    wide, narrow = cols // n, cols // n // parts
+def finish(base, received):
+    rows, cols = base.shape
+    some = rows // 4 if rows % 64 == 0 else rows
     return pl.pallas_call(
-        functools.partial(finish_kernel, parts, len(terms[0]) - 1),
-        grid=(n,),
+        finish_kernel,
+        grid=(rows // some,),
         out_shape=jax.ShapeDtypeStruct((rows, cols), jnp.float32),
-        in_specs=[pl.BlockSpec((rows, wide), lambda f: (0, f))]
-        + [pl.BlockSpec((rows, narrow), lambda f: (0, f))] * sum(len(t) for t in terms),
-        out_specs=pl.BlockSpec((rows, wide), lambda f: (0, f)),
+        in_specs=[pl.BlockSpec((some, cols), lambda r: (r, 0))]
+        + [pl.BlockSpec((some, cols // CHUNKS), lambda r: (r, 0))] * len(received),
+        out_specs=pl.BlockSpec((some, cols), lambda r: (r, 0)),
         compiler_params=pltpu.CompilerParams(vmem_limit_bytes=16 * 1024 * 1024),
         name="finish",
-    )(own_rows, *[term for some in terms for term in some])
+    )(base, *received)
 
 
 def shards(
@@ -239,10 +245,8 @@
     scale = lax.rsqrt(jnp.mean(widened * widened, axis=1, keepdims=True) + EPSILON)
     normed = (widened * scale * norm_gain[None, :]).astype(jnp.bfloat16)
 
-    part_cols = w_out.shape[1] // PARTS
-    own_parts = [w_out[:, part * part_cols : (part + 1) * part_cols] for part in range(PARTS)]
-    weights, own_parts = lax.optimization_barrier((weights, own_parts))
-    out_parts = [lax.all_gather(part, "fsdp", axis=1, tiled=True) for part in own_parts]
+    weights, w_out = lax.optimization_barrier((weights, w_out))
+    w_out = lax.all_gather(w_out, "fsdp", axis=1, tiled=True)
 
     pairs = jnp.dot(normed, weights[:, : 2 * key_cols], preferred_element_type=jnp.float32)
     pairs = pairs + jnp.concatenate([key_bias, value_bias]).astype(jnp.float32)[None, :]
@@ -262,21 +266,23 @@
     me = lax.axis_index("tp")
     own_rows = lax.dynamic_slice_in_dim(hidden, me * share, share, 0)
     own_attended = lax.dynamic_slice_in_dim(attended, me * share, share, 0)
-    terms = []
-    for part in range(PARTS):
-        some = []
-        for d in range(1, tp):
-            peer = lax.rem(me + d, tp)
-            rows = lax.dynamic_slice_in_dim(attended, peer * share, share, 0)
-            term = jnp.dot(rows, out_parts[part], preferred_element_type=jnp.float32)
-            some.append(
+    width = w_out.shape[1] // CHUNKS
+    received = []
+    for d in range(1, tp):
+        rows = lax.dynamic_slice_in_dim(attended, lax.rem(me + d, tp) * share, share, 0)
+        for chunk in range(CHUNKS):
+            term = jnp.dot(
+                rows,
+                w_out[:, chunk * width : (chunk + 1) * width],
+                preferred_element_type=jnp.float32,
+            )
+            received.append(
                 lax.ppermute(
                     term.astype(jnp.bfloat16), "tp", [(i, (i + d) % tp) for i in range(tp)]
                 )
             )
-        some.append(jnp.dot(own_attended, out_parts[part], preferred_element_type=jnp.float32))
-        terms.append(some)
-    return finish(own_rows, terms, n)
+    base = jnp.dot(own_attended, w_out, preferred_element_type=jnp.float32)
+    return finish(base + own_rows.astype(jnp.float32), received)
 
 
 def solution(mesh):

time: 573 us -> 476 us (0.83)
  waiting for transfers between devices: 396 us -> 300 us
  matrix products: 51.4 us -> 62.7 us
  Pallas kernels: 83.9 us -> 73.7 us
    all_gather x2 -> x1, waiting for transfers between devices: 174 us -> 78.3 us  [shards(): w_out = lax.all_gather(w_out, 'fsdp', axis=1, tiled=True)]
    dot_general x4 -> x5, matrix products: 27.9 us -> 37.6 us  [the longest x4 21.7 us: shards(): jnp.dot(rows, w_out[:, chunk * width:(chunk + 1) * width], preferred_elem...]
    pallas_call x1, Pallas kernels: 9.66 us -> 2.46 us  [finish(): pl.pallas_call(finish_kernel, grid=(rows // some,), out_shape=jax.ShapeDt...]
    ppermute x2 -> x4, waiting for transfers between devices: 12.6 us -> 11.8 us  [shards(): lax.ppermute(term.astype(jnp.bfloat16), 'tp', [(i, (i + d) % tp) for i in...]
  transfers between devices with their start and end apart: 5 -> 6, of which waited for: 4 -> 4; matrix products, arithmetic and copies ran while one was open for 11% -> 14% of each run, Pallas kernels for 13% -> 15%
where the time goes in v2:
time: 476 us
  waiting for transfers between devices  300 us (63%)
  Pallas kernels  73.7 us (15%)
  matrix products  62.7 us (13%)
  between operations  18.7 us (4%)
  other arithmetic  9.53 us (2%)
  local copies, waits for them, and re-layouts  6.69 us (1%)
    all_gather x1, waiting for transfers between devices, shards(): lax.all_gather(jnp.concatenate([key_part, value_part, w_query], axis=1),...  210 us
    all_gather x1, waiting for transfers between devices, shards(): w_out = lax.all_gather(w_out, 'fsdp', axis=1, tiled=True)  78.3 us
    pallas_call x1, Pallas kernels, gather_blocks(): pl.pallas_call(functools.partial(gather_kernel, n), out_shape=jax.ShapeDt...  57 us
    dot_general x4, matrix products, shards(): jnp.dot(rows, w_out[:, chunk * width:(chunk + 1) * width], preferred_elem...  21.7 us
    dot_general x1, matrix products, shards(): jnp.dot(normed, weights[:, 2 * key_cols:], preferred_element_type=jnp.flo...  18 us
    dot_general x1, matrix products, shards(): base = jnp.dot(own_attended, w_out, preferred_element_type=jnp.float32)  15.8 us
    pallas_call x1, Pallas kernels, attend(): pl.pallas_call(functools.partial(attend_kernel, block), grid=(heads,), ou...  14.2 us
    ppermute x4, waiting for transfers between devices, shards(): lax.ppermute(term.astype(jnp.bfloat16), 'tp', [(i, (i + d) % tp) for i in...  11.8 us
  transfers between devices with their start and end apart: 6, of which 4 were waited for; matrix products, arithmetic and copies ran while one was open for 14% of the time, Pallas kernels for 15%

profile of v2, /device:TPU:0, one launch (start us, length us, event | category | flops | bytes accessed | tf_op | source)
XLA Modules:
  0.0 475.9 jit_solution(9919990032125383516)
XLA Ops:
  6.5 0.0 all-gather.3.cloned.1.call-start
  6.6 1.1 constant_dynamic-slice_fusion
  7.7 3.3 pad_maximum_fusion
  10.9 0.0 all-gather.3.cloned.1.call-update
  11.0 0.0 all-gather.5.cloned.1.call-start
  11.0 210.4 %all-gather.3.cloned.1.call-done = bf16[8192,2560]{1,0:T(8,128)(2,1)} async-done(((bf16[512,2560]{1,0:T(8,128)(2,1)}), bf16[8192,2560]{1,0:T(8,128)(2,1)}) %all-gather.3.cloned.1.call-update) | async-done | bytes 41943056 | tf_op jit(solution)/shard_map/all_gather | solution.py:237
  221.4 0.0 all-gather.5.cloned.1.call-update
  221.4 0.0 copy-done.7
  221.4 0.2 reduce-window.8
  221.6 0.1 convert_reduce_fusion
  221.7 0.1 select_reduce_fusion
  221.8 0.6 slice.50
  224.3 0.5 slice.51
  228.0 0.0 copy-done.5
  228.0 0.1 dynamic_slice.23
  228.1 0.0 copy-done.6
  228.1 0.1 dynamic_slice.24
  228.2 0.1 copy.12.begin_ref
  228.4 0.1 pad_add_fusion.reach_ref
  228.5 4.2 fusion.2
  232.7 0.5 fusion.44
  233.2 0.0 copy-done.4
  233.2 7.1 %fusion.30 = f32[256,512]{1,0:T(8,128)S(1)} fusion(bf16[8192,2560]{1,0:T(8,128)(2,1)} %all-gather.3.cloned.1.call-done, bf16[256,8192]{1,0:T(8,128)(2,1)} %param.10, f32[8192]{0:T(1024)S(1)} %copy-done.4, f32[256]{0:T(256)S(1)} %add_rsqrt_fusion, f32[512]{0:T(512)S(1)} %maximum_convert_fusion), kind=kOutput, calls=%fused_computation.24 | convolution fusion | flops 2156003328 | bytes 13143040 | tf_op jit(solution)/shard_map/dot_general | solution.py:251
  240.4 0.1 fusion.50
  240.5 0.2 fusion.43
  240.7 0.1 fusion.41
  240.8 0.7 pad_maximum_fusion.1.block_ref
  241.6 57.0 %kv_gather.1 = bf16[16,256,512]{2,1,0:T(8,128)(2,1)} custom-call(bf16[256,512]{1,0:T(8,128)(2,1)} %pad_maximum_fusion.1.block_ref), custom_call_target="tpu_custom_call" | custom-call | bytes 100000000 | tf_op jit(solution)/shard_map/kv_gather/pallas_call | solution.py:103
  298.6 18.0 %fusion.15.query_ref = f32[256,2048]{1,0:T(8,128)} fusion(bf16[8192,2560]{1,0:T(8,128)(2,1)} %all-gather.3.cloned.1.call-done, bf16[256,8192]{1,0:T(8,128)(2,1)} %param.10, f32[8192]{0:T(1024)S(1)} %copy-done.4, f32[256]{0:T(256)S(1)} %add_rsqrt_fusion, f32[2048]{0:T(1024)S(1)} %convert_element_type.45), kind=kOutput, calls=%fused_computation.18 | convolution fusion | flops 8598847488 | bytes 39887872 | tf_op jit(solution)/shard_map/dot_general | solution.py:260
  316.6 2.4 copy-done
  319.0 1.6 copy-done.2
  320.6 14.2 %attend.1 = bf16[256,2048]{1,0:T(8,128)(2,1)S(1)} custom-call(s32[2]{0:T(128)S(1)} %pad_add_fusion.reach_ref, f32[256,2048]{1,0:T(8,128)S(1)} %copy-done.2, f32[256,128]{1,0:T(8,128)S(1)} %get-tuple-element.16.cos_ref, f32[256,128]{1,0:T(8,128)S(1)} %get-tuple-element.10.sin_ref, s32[256,1]{1,0:T(8,128)S(1)} %copy.12.begin_ref, ...), custom_call_target="tpu_custom_call" | custom-call | flops 8589934592 | bytes 100000000 | tf_op jit(solution)/shard_map/attend/pallas_call | solution.py:170
  334.9 0.0 copy-start.1
  334.9 78.3 %all-gather.5.cloned.1.call-done = bf16[2048,8192]{1,0:T(8,128)(2,1)} async-done(((bf16[2048,512]{1,0:T(8,128)(2,1)}), bf16[2048,8192]{1,0:T(8,128)(2,1)}) %all-gather.5.cloned.1.call-update) | async-done | bytes 33554448 | tf_op jit(solution)/shard_map/all_gather | solution.py:249
  413.2 5.4 %fusion.18 = bf16[128,2048]{1,0:T(8,128)(2,1)} fusion(bf16[2048,8192]{1,0:T(8,128)(2,1)} %all-gather.5.cloned.1.call-done, bf16[256,2048]{1,0:T(8,128)(2,1)S(1)} %attend.1, s32[]{:T(128)S(6)} %select_n.34), kind=kOutput, calls=%fused_computation.20 | convolution fusion | flops 1074003968 | bytes 9437188 | tf_op jit(solution)/shard_map/dot_general | solution.py:274
  418.6 1.5 collective-permute-start
  420.1 5.4 %fusion.21 = bf16[128,2048]{1,0:T(8,128)(2,1)} fusion(bf16[2048,8192]{1,0:T(8,128)(2,1)} %all-gather.5.cloned.1.call-done, bf16[256,2048]{1,0:T(8,128)(2,1)S(1)} %attend.1, s32[]{:T(128)S(6)} %select_n.34), kind=kOutput, calls=%fused_computation.21 | convolution fusion | flops 1074003968 | bytes 9437188 | tf_op jit(solution)/shard_map/dot_general | solution.py:274
  425.5 0.6 collective-permute-start.1
  426.0 5.5 %fusion.24 = bf16[128,2048]{1,0:T(8,128)(2,1)} fusion(bf16[2048,8192]{1,0:T(8,128)(2,1)} %all-gather.5.cloned.1.call-done, bf16[256,2048]{1,0:T(8,128)(2,1)S(1)} %attend.1, s32[]{:T(128)S(6)} %select_n.34), kind=kOutput, calls=%fused_computation.22 | convolution fusion | flops 1074003968 | bytes 9437188 | tf_op jit(solution)/shard_map/dot_general | solution.py:274
  431.5 1.5 collective-permute-start.2
  433.0 5.4 %fusion.27 = bf16[128,2048]{1,0:T(8,128)(2,1)} fusion(bf16[2048,8192]{1,0:T(8,128)(2,1)} %all-gather.5.cloned.1.call-done, bf16[256,2048]{1,0:T(8,128)(2,1)S(1)} %attend.1, s32[]{:T(128)S(6)} %select_n.34), kind=kOutput, calls=%fused_computation.23 | convolution fusion | flops 1074003968 | bytes 9437188 | tf_op jit(solution)/shard_map/dot_general | solution.py:274
  438.4 0.6 collective-permute-start.3
  439.0 15.8 %convolution_add_fusion.base_ref = f32[128,8192]{1,0:T(8,128)S(1)} fusion(bf16[2048,8192]{1,0:T(8,128)(2,1)} %all-gather.5.cloned.1.call-done, bf16[256,8192]{1,0:T(8,128)(2,1)} %param.10, s32[]{:T(128)S(6)} %select_n.33, bf16[256,2048]{1,0:T(8,128)(2,1)} %copy-done.1), kind=kOutput, calls=%fused_computation.4 | convolution fusion | flops 4297064448 | bytes 40371200 | tf_op jit(solution)/shard_map/dot_general | solution.py:284
  454.8 0.0 collective-permute-done.refs_0_
  454.8 0.0 collective-permute-done.1.refs_1_
  454.8 1.2 collective-permute-done.2.refs_2_
  456.1 10.5 %collective-permute-done.3.refs_3_ = bf16[128,2048]{1,0:T(8,128)(2,1)S(1)} collective-permute-done((bf16[128,2048]{1,0:T(8,128)(2,1)}, bf16[128,2048]{1,0:T(8,128)(2,1)S(1)}, u32[]{:S(2)}, u32[]{:S(2)}) %collective-permute-start.3) | collective-permute-done | bytes 524320 | tf_op jit(solution)/shard_map/ppermute | solution.py:280
  466.6 2.5 finish.1
  (18 shorter events, 0.1 us)
Async XLA Ops:
  6.5 214.9 %copy-start.7 = (s32[4]{0:T(128)S(1)}, s32[4]{0:T(128)}, u32[]{:S(2)}) copy-start(s32[4]{0:T(128)} %param.19) | copy-start | bytes 52
  6.5 221.5 %copy-start.5 = (bf16[512]{0:T(512)(128)(2,1)S(1)}, bf16[512]{0:T(512)(128)(2,1)}, u32[]{:S(2)}) copy-start(bf16[512]{0:T(512)(128)(2,1)} %param.16) | copy-start | bytes 3076
  6.5 221.6 %copy-start.6 = (bf16[512]{0:T(512)(128)(2,1)S(1)}, bf16[512]{0:T(512)(128)(2,1)}, u32[]{:S(2)}) copy-start(bf16[512]{0:T(512)(128)(2,1)} %param.17) | copy-start | bytes 3076
  6.5 221.6 %copy-start.3 = (bf16[2048]{0:T(1024)(128)(2,1)S(1)}, bf16[2048]{0:T(1024)(128)(2,1)}, u32[]{:S(2)}) copy-start(bf16[2048]{0:T(1024)(128)(2,1)} %param.15) | copy-start | bytes 12292
  6.5 226.7 %copy-start.4 = (f32[8192]{0:T(1024)S(1)}, f32[8192]{0:T(1024)}, u32[]{:S(2)}) copy-start(f32[8192]{0:T(1024)} %param.11) | copy-start | bytes 98308
  6.5 214.9 %all-gather.3.cloned.1.call-start = ((), (), s32[]{:S(2)}) async-start(), calls=%async_computation | async-start | bytes 44564480 | tf_op jit(solution)/shard_map/all_gather | solution.py:237
  11.0 402.2 %all-gather.5.cloned.1.call-start = ((), (), s32[]{:S(2)}) async-start(), calls=%async_computation.1 | async-start | bytes 35651584 | tf_op jit(solution)/shard_map/all_gather | solution.py:249
  316.6 2.5 copy-start
  319.0 1.6 copy-start.2
  334.9 98.1 %copy-start.1 = (bf16[256,2048]{1,0:T(8,128)(2,1)}, bf16[256,2048]{1,0:T(8,128)(2,1)S(1)}, u32[]{:S(2)}) copy-start(bf16[256,2048]{1,0:T(8,128)(2,1)S(1)} %attend.1) | copy-start | bytes 3145732
  418.6 36.2 %collective-permute-start = (bf16[128,2048]{1,0:T(8,128)(2,1)}, bf16[128,2048]{1,0:T(8,128)(2,1)S(1)}, u32[]{:S(2)}, u32[]{:S(2)}) collective-permute-start(bf16[128,2048]{1,0:T(8,128)(2,1)} %fusion.18), channel_id=1, source_target_pairs={{0,1},{1,0},{2,3},{3,2},{4,5},{5,4},{6,7},{7,6},{8,9},{9,8},{10,11... | collective-permute-start | bytes 1572872 | tf_op jit(solution)/shard_map/ppermute | solution.py:280
  425.5 29.4 %collective-permute-start.1 = (bf16[128,2048]{1,0:T(8,128)(2,1)}, bf16[128,2048]{1,0:T(8,128)(2,1)S(1)}, u32[]{:S(2)}, u32[]{:S(2)}) collective-permute-start(bf16[128,2048]{1,0:T(8,128)(2,1)} %fusion.21), channel_id=1, source_target_pairs={{0,1},{1,0},{2,3},{3,2},{4,5},{5,4},{6,7},{7,6},{8,9},{9,8},{10,11... | collective-permute-start | bytes 1572872 | tf_op jit(solution)/shard_map/ppermute | solution.py:280
  431.5 24.6 %collective-permute-start.2 = (bf16[128,2048]{1,0:T(8,128)(2,1)}, bf16[128,2048]{1,0:T(8,128)(2,1)S(1)}, u32[]{:S(2)}, u32[]{:S(2)}) collective-permute-start(bf16[128,2048]{1,0:T(8,128)(2,1)} %fusion.24), channel_id=1, source_target_pairs={{0,1},{1,0},{2,3},{3,2},{4,5},{5,4},{6,7},{7,6},{8,9},{9,8},{10,11... | collective-permute-start | bytes 1572872 | tf_op jit(solution)/shard_map/ppermute | solution.py:280
  438.4 28.2 %collective-permute-start.3 = (bf16[128,2048]{1,0:T(8,128)(2,1)}, bf16[128,2048]{1,0:T(8,128)(2,1)S(1)}, u32[]{:S(2)}, u32[]{:S(2)}) collective-permute-start(bf16[128,2048]{1,0:T(8,128)(2,1)} %fusion.27), channel_id=1, source_target_pairs={{0,1},{1,0},{2,3},{3,2},{4,5},{5,4},{6,7},{7,6},{8,9},{9,8},{10,11... | collective-permute-start | bytes 1572872 | tf_op jit(solution)/shard_map/ppermute | solution.py:280
Sparse Core Ops, SparseCore 0:
  11.1 210.2 all-gather.2
  223.0 190.1 all-gather.4
